TPU v7x, 32 devices: a whole 2x2x4 slice. The times are simulated.
32 devices in a mesh: dp: 8 (over y, x, core), pipe: 4 (over z).
Axes of the slice: x: 2, y: 2, z: 4, core: 2. Of those that a mesh axis runs over, the one named last changes fastest.
Arguments:
- embed_grad: bfloat16 [512, 4608], P('dp', 'pipe'), may hold values from -0.35 to 0.35
- ids: int32 [512], P('dp'), may hold values from 0 to 11263
Outputs:
- table_grad: float32 [11264, 4608], P('dp', 'pipe')
All inputs are finite; a program needn't handle non-finite values.
Results may differ from a plain program's by a relative error of at most 0.00035.
Values may be sent and summed in bfloat16 or wider, within the bound.
A program may use at most 64 MiB of HBM per device.

v0:
```python
import functools
import math

import jax
import jax.numpy as jnp
from jax import lax
from jax.experimental import pallas as pl
from jax.experimental.pallas import tpu as pltpu
from jax.sharding import PartitionSpec as P

VOC_DEV = 1408
CHUNKS = 4
STRIPES = 8
MESH = pl.DeviceIdType.MESH


def gather_kernel(n_dp, n_pipe, clip, scale, grad_ref, ids_ref, all_ref, row_ref, factor_ref,
                  held, id_held, sums, load_sem, send_sem, recv_sem, sum_send, sum_recv):
    me = lax.axis_index("dp")
    z = lax.axis_index("pipe")
    core = lax.rem(me, 2)
    to_sibling = 1 - 2 * core
    to_x = 2 - 4 * lax.rem(me // 2, 2)
    to_y = 4 - 8 * (me // 4)
    sibling, x_peer, y_peer = me + to_sibling, me + to_x, me + to_y
    diagonal = me + to_x + to_y
    relayed = me + (1 - core) * to_x + core * to_y
    relay_to = me + core * to_x + (1 - core) * to_y
    rows = held.shape[1] // CHUNKS

    load = pltpu.make_async_copy(grad_ref, held.at[me], load_sem.at[0])
    load.start()
    load_ids = pltpu.make_async_copy(ids_ref, id_held.at[me], load_sem.at[1])
    load_ids.start()

    barrier = pltpu.get_barrier_semaphore()
    for peer in (sibling, x_peer, y_peer):
        pl.semaphore_signal(barrier, inc=1, device_id=(peer, z), device_id_type=MESH)
    for step in range(1, n_pipe):
        pl.semaphore_signal(
            barrier, inc=1, device_id=(me, lax.rem(z + step, n_pipe)), device_id_type=MESH
        )
    pl.semaphore_wait(barrier, 3 + n_pipe - 1)
    load_ids.wait()
    load.wait()

    def piece(block, part):
        if part == 0:
            return id_held.at[block]
        return held.at[block, pl.ds((part - 1) * rows, rows)]

    def copy(block, part, target, kind):
        return pltpu.make_async_remote_copy(
            src_ref=piece(block, part), dst_ref=piece(block, part),
            send_sem=send_sem.at[kind, part], recv_sem=recv_sem.at[block, part],
            device_id=(target, z), device_id_type=MESH,
        )

    sent = []

    def send(block, part, target, kind):
        moving = copy(block, part, target, kind)
        moving.start()
        sent.append(moving)

    def arrived(block, part):
        copy(block, part, sibling, 0).wait_recv()

    parts = range(CHUNKS + 1)
    for part in parts:
        send(me, part, relay_to, 0)
        send(me, part, relayed, 1)
        send(me, part, sibling, 2)
    for part in parts:
        arrived(relayed, part)
        send(relayed, part, relay_to, 3)
        send(relayed, part, sibling, 4)
        arrived(relay_to, part)
        send(relay_to, part, sibling, 5)
    arrived(diagonal, 0)
    send(diagonal, 0, sibling, 6)
    for block in (sibling, sibling + to_x, sibling + to_y, sibling + to_x + to_y):
        arrived(block, 0)

    ids = jnp.concatenate([id_held[block] for block in range(n_dp)], axis=1)
    row_ref[...] = ids
    tokens = ids.shape[1]
    columns = []
    for start in range(0, tokens, 128):
        columns.append(
            jnp.broadcast_to(ids[:, start:start + 128].astype(jnp.float32), (128, 128)).T[:, :1]
        )
    column = jnp.concatenate(columns, axis=0)
    same = jnp.where(column == ids.astype(jnp.float32), 1.0, 0.0)
    here = lax.broadcasted_iota(jnp.int32, same.shape, 0)
    other = lax.broadcasted_iota(jnp.int32, same.shape, 1)
    earlier = jnp.sum(jnp.where(other < here, same, 0.0), axis=1, keepdims=True)
    first = jnp.where(earlier == 0.0, same, 0.0).astype(jnp.bfloat16)

    for part in parts[1:]:
        arrived(diagonal, part)
        send(diagonal, part, sibling, 6)
    for block in (sibling, sibling + to_x, sibling + to_y, sibling + to_x + to_y):
        for part in parts[1:]:
            arrived(block, part)

    width = held.shape[2]
    total = jnp.zeros((1, 128), jnp.float32)
    tile = 384 if width % 384 == 0 else 128
    for start in range(0, width, tile):
        block = held[:, :, start:start + tile].reshape(tokens, tile)
        summed = jnp.dot(first, block, preferred_element_type=jnp.float32)
        squares = jnp.sum(summed * summed, axis=0, keepdims=True)
        for lane in range(0, tile, 128):
            total = total + squares[:, lane:lane + 128]
    sums[z] = total
    shares = []
    for step in range(1, n_pipe):
        share = pltpu.make_async_remote_copy(
            src_ref=sums.at[z], dst_ref=sums.at[z],
            send_sem=sum_send.at[step], recv_sem=sum_recv.at[z],
            device_id=(me, lax.rem(z + step, n_pipe)), device_id_type=MESH,
        )
        share.start()
        shares.append(share)
    all_ref[...] = held[...]
    for step in range(1, n_pipe):
        origin = lax.rem(z + step, n_pipe)
        pltpu.make_async_remote_copy(
            src_ref=sums.at[origin], dst_ref=sums.at[origin],
            send_sem=sum_send.at[step], recv_sem=sum_recv.at[origin],
            device_id=(me, origin), device_id_type=MESH,
        ).wait_recv()
    whole = sums[0]
    for index in range(1, n_pipe):
        whole = whole + sums[index]
    norm = jnp.sqrt(jnp.sum(whole, axis=1, keepdims=True) * (scale * scale) + 1e-06)
    factor = jnp.minimum(1.0, clip / norm) * scale
    factor_ref[...] = jnp.broadcast_to(factor, factor_ref.shape)
    for moving in sent:
        moving.wait_send()
    for share in shares:
        share.wait_send()


def rows_kernel(ids_ref, factor_ref, all_ref, out_ref, made, sem):
    height = made.shape[0] // STRIPES
    tokens = ids_ref.shape[1]
    offset = lax.axis_index("dp") * VOC_DEV
    block = all_ref[...].reshape(tokens, all_ref.shape[2])
    factor = factor_ref[:, :1]
    writes = []
    for stripe in range(STRIPES):
        where = pl.ds(stripe * height, height)
        wanted = lax.broadcasted_iota(jnp.int32, (height, tokens), 0) + (offset + stripe * height)
        hot = jnp.where(wanted == ids_ref[...], 1.0, 0.0).astype(jnp.bfloat16)
        made[where] = jnp.dot(hot, block, preferred_element_type=jnp.float32) * factor
        write = pltpu.make_async_copy(made.at[where], out_ref.at[where], sem.at[stripe])
        write.start()
        writes.append(write)
    for write in writes:
        write.wait()


def rows_of(all_grads, ids, factor):
    n_dp, count, width = all_grads.shape
    vmem = pl.BlockSpec(memory_space=pltpu.VMEM)
    return pl.pallas_call(
        rows_kernel,
        out_shape=jax.ShapeDtypeStruct((VOC_DEV, width), jnp.float32),
        in_specs=[vmem, vmem, vmem],
        out_specs=pl.BlockSpec(memory_space=pltpu.HBM),
        scratch_shapes=[
            pltpu.VMEM((VOC_DEV, width), jnp.float32),
            pltpu.SemaphoreType.DMA((STRIPES,)),
        ],
        compiler_params=pltpu.CompilerParams(vmem_limit_bytes=24 * 2**20),
        name="rows",
    )(ids, factor, all_grads)


def per_device(embed_grad, ids):
    n_dp, n_pipe = lax.axis_size("dp"), lax.axis_size("pipe")
    count, width = embed_grad.shape
    features = width * n_pipe
    tokens = count * n_dp
    vmem = pl.BlockSpec(memory_space=pltpu.VMEM)
    hbm = pl.BlockSpec(memory_space=pltpu.HBM)
    all_grads, all_ids, factor = pl.pallas_call(
        functools.partial(
            gather_kernel, n_dp, n_pipe, 0.2 * math.sqrt(tokens * features), math.sqrt(features)
        ),
        out_shape=(
            pltpu.VMEM((n_dp, count, width), embed_grad.dtype),
            pltpu.VMEM((1, tokens), jnp.int32),
            pltpu.VMEM((1, 128), jnp.float32),
        ),
        in_specs=[hbm, hbm],
        out_specs=(vmem, vmem, vmem),
        scratch_shapes=[
            pltpu.VMEM((n_dp, count, width), embed_grad.dtype),
            pltpu.VMEM((n_dp, 1, count), jnp.int32),
            pltpu.VMEM((n_pipe, 1, 128), jnp.float32),
            pltpu.SemaphoreType.DMA((2,)),
            pltpu.SemaphoreType.DMA((7, CHUNKS + 1)),
            pltpu.SemaphoreType.DMA((n_dp, CHUNKS + 1)),
            pltpu.SemaphoreType.DMA((n_pipe,)),
            pltpu.SemaphoreType.DMA((n_pipe,)),
        ],
        compiler_params=pltpu.CompilerParams(
            collective_id=0, has_side_effects=True, vmem_limit_bytes=24 * 2**20
        ),
        name="gather",
    )(
        pltpu.with_memory_space_constraint(embed_grad, pltpu.HBM),
        pltpu.with_memory_space_constraint(ids.reshape(1, count), pltpu.HBM),
    )
    return rows_of(all_grads, all_ids, factor)


def per_device_any(embed_grad, ids):
    tokens_all = embed_grad.shape[0] * lax.axis_size("dp")
    features = embed_grad.shape[1] * lax.axis_size("pipe")
    offset = lax.axis_index("dp") * VOC_DEV
    cotangent_all = lax.all_gather(embed_grad, "dp", axis=0, tiled=True)
    local = lax.all_gather(ids, "dp", axis=0, tiled=True) - offset
    inside = (local >= 0) & (local < VOC_DEV)
    segment = jnp.where(inside, local, VOC_DEV).astype(jnp.int32)
    summed = jax.ops.segment_sum(cotangent_all.astype(jnp.float32), segment, VOC_DEV + 1)
    grad_rows = summed[:VOC_DEV] * math.sqrt(features)
    total = lax.psum(jnp.sum(grad_rows * grad_rows), ("dp", "pipe"))
    grad_norm = jnp.sqrt(total + 1e-06)
    return grad_rows * jnp.minimum(1.0, 0.2 * math.sqrt(tokens_all * features) / grad_norm)


def solution(mesh):
    placed = (P("dp", "pipe"), P("dp"))
    cube = mesh.shape["dp"] == 2 * 2 * 2
    return jax.shard_map(
        per_device if cube else per_device_any, mesh=mesh, in_specs=placed,
        out_specs=P("dp", "pipe"), check_vma=False,
    )
```

profile of v0, /device:TPU:0, one launch (start us, length us, event | category | flops | bytes accessed | tf_op | source)
XLA Modules:
  0.0 22.3 jit_solution(17656098229324599650)
XLA Ops:
  0.0 19.1 %gather.1 = (bf16[8,64,1152]{2,1,0:T(8,128)(2,1)S(1)}, s32[1,512]{1,0:T(1,128)S(1)}, f32[1,128]{1,0:T(1,128)S(1)}) custom-call(bf16[64,1152]{1,0:T(8,128)(2,1)} %grad_ref.1, s32[1,64]{1,0:T(1,128)} %bitcast.1), custom_call_target="tpu_custom_call" | custom-call | tf_op jit(solution)/shard_map/gather/pallas_call | solution.py:189
  19.1 3.2 %rows.1 = f32[1408,1152]{1,0:T(8,128)} custom-call(s32[1,512]{1,0:T(1,128)S(1)} %get-tuple-element.8.ids_ref, f32[1,128]{1,0:T(1,128)S(1)} %get-tuple-element.9.factor_ref, bf16[8,64,1152]{2,1,0:T(8,128)(2,1)S(1)} %get-tuple-element.10.all_ref), custom_call_target="tpu_custom_call" | custom-call | tf_op jit(solution)/shard_map/rows/pallas_call | solution.py:168
where the time goes:
time: 22.5 us; the launch traced here: 22.3 us
  Pallas kernels  22.3 us (99%)
    pallas_call x1, Pallas kernels, per_device(): pl.pallas_call(functools.partial(gather_kernel, n_dp, n_pipe, 0.2 * math....  19.1 us
    pallas_call x1, Pallas kernels, rows_of(): pl.pallas_call(rows_kernel, out_shape=jax.ShapeDtypeStruct((VOC_DEV, widt...  3.21 us

commit v1 on v0

v1 whole, which is shorter than its diff:
```python
import functools
import math

import jax
import jax.numpy as jnp
from jax import lax
from jax.experimental import pallas as pl
from jax.experimental.pallas import tpu as pltpu
from jax.sharding import PartitionSpec as P

VOC_DEV = 1408
CHUNKS = 3
STRIPES = 8
MESH = pl.DeviceIdType.MESH


def gather_kernel(n_dp, n_pipe, clip, scale, grad_ref, ids_ref, made_ref, factor_ref,
                  held, id_held, gathered, first, hot, sums, load_sem, late_sem, far_sem, line_sem,
                  send_sem, recv_sem, id_sem, part_sem, sum_sem):
    me = lax.axis_index("dp")
    z = lax.axis_index("pipe")
    chip, core = me // 2, lax.rem(me, 2)
    to_sibling = 1 - 2 * core
    to_x = 2 - 4 * lax.rem(chip, 2)
    to_y = 4 - 8 * (chip // 2)
    sibling, x_peer, y_peer = me + to_sibling, me + to_x, me + to_y
    diagonal = me + to_x + to_y
    relayed = me + (1 - core) * to_x + core * to_y
    relay_to = me + core * to_x + (1 - core) * to_y
    chunks, _, count, tile = held.shape
    tokens = n_dp * count
    last_chip = n_dp // 2 - 1
    late = chip == last_chip
    collects = (core == 1) & (chip < chunks)

    def collector(part):
        return 2 * part + 1

    load_ids = pltpu.make_async_copy(ids_ref, id_held.at[me], load_sem.at[0])
    load_ids.start()
    for part in range(chunks):
        columns = grad_ref.at[:, pl.ds(part * tile, tile)]
        pltpu.make_async_copy(columns, held.at[part, me], load_sem.at[1]).start()
        pl.when(me == collector(part))(
            pltpu.make_async_copy(columns, gathered.at[me], part_sem.at[1]).start
        )

    def taken(ref, semaphore):
        pltpu.make_async_copy(ref, ref, semaphore).wait()

    barrier = pltpu.get_barrier_semaphore()

    def greet(semaphore, device, plane):
        pl.semaphore_signal(semaphore, inc=1, device_id=(device, plane), device_id_type=MESH)

    greet(barrier, sibling, z)

    @pl.when(chip < last_chip)
    def _():
        for ahead in range(2, n_dp, 2):
            for other in range(2):
                greet(barrier, lax.rem(2 * chip + ahead, n_dp) + other, z)

    for other in range(1, n_pipe):
        @pl.when(z < other)
        def _():
            greet(barrier, me, other)
    with jax.named_scope("barrier"):
        pl.semaphore_wait(barrier, jnp.where(late, n_dp - 1, n_dp - 3) + z)
    load_ids.wait()

    @pl.when(late)
    def _():
        for other in range(n_dp - 2):
            greet(late_sem, other, z)

    for other in range(n_pipe - 1):
        @pl.when(z > other)
        def _():
            greet(far_sem, me, other)

    def id_copy(ahead):
        return pltpu.make_async_remote_copy(
            src_ref=id_held.at[me], dst_ref=id_held.at[me],
            send_sem=id_sem.at[0], recv_sem=id_sem.at[1],
            device_id=(lax.rem(me + ahead, n_dp), z), device_id_type=MESH,
        )

    for ahead in range(1, n_dp):
        early = (lax.rem(me + ahead, n_dp) // 2 < last_chip) | late
        pl.when(early)(lambda ahead=ahead: id_copy(ahead).start())

    def part_copy(part):
        return pltpu.make_async_remote_copy(
            src_ref=held.at[part, me], dst_ref=gathered.at[me],
            send_sem=part_sem.at[0], recv_sem=part_sem.at[1],
            device_id=(collector(part), z), device_id_type=MESH,
        )

    taken(held.at[:, me], load_sem.at[1])
    for part in range(chunks):
        pl.when(me != collector(part))(lambda part=part: part_copy(part).start())

    def copy(block, part, target, place):
        return pltpu.make_async_remote_copy(
            src_ref=held.at[part, block], dst_ref=held.at[part, block],
            send_sem=send_sem.at[0], recv_sem=recv_sem.at[place, part],
            device_id=(target, z), device_id_type=MESH,
        )

    def arrived(place, part, count=1):
        taken(held.at[part, pl.ds(0, count)], recv_sem.at[place, part])

    own = [(relay_to, 0), (relayed, 1)]

    def send_own(part):
        for target, place in own:
            pl.when(late | (target // 2 < last_chip))(copy(me, part, target, place).start)

    def send_late(part):
        for target, place in own:
            pl.when(target // 2 == last_chip)(copy(me, part, target, place).start)

    send_own(0)
    with jax.named_scope("late"):
        @pl.when(chip < last_chip)
        def _():
            pl.semaphore_wait(late_sem, 2)
            for ahead in range(1, n_dp):
                pl.when(lax.rem(me + ahead, n_dp) // 2 == last_chip)(
                    lambda ahead=ahead: id_copy(ahead).start()
                )
            send_late(0)
    for part in range(1, chunks):
        send_own(part)
        pl.when(chip < last_chip)(lambda part=part: send_late(part))
    for part in range(chunks):
        copy(me, part, sibling, 3).start()

    with jax.named_scope("far"):
        @pl.when(z < n_pipe - 1)
        def _():
            pl.semaphore_wait(far_sem, n_pipe - 1 - z)
    for part in range(chunks):
        pl.when(me != collector(part))(lambda part=part: greet(line_sem, collector(part), z))

    with jax.named_scope("ids"):
        taken(id_held.at[pl.ds(0, n_dp - 1)], id_sem.at[1])
    ids = jnp.concatenate([id_held[block] for block in range(n_dp)], axis=1)

    def sum_copy(ahead, up, slot):
        return pltpu.make_async_remote_copy(
            src_ref=sums.at[slot], dst_ref=sums.at[slot],
            send_sem=sum_sem.at[0], recv_sem=sum_sem.at[1],
            device_id=(lax.rem(me + ahead, n_dp), lax.rem(z + up, n_pipe)), device_id_type=MESH,
        )

    targets = [
        (ahead, up % n_pipe) for up in range(1, n_pipe + 1) for ahead in range(n_dp)
        if ahead or up < n_pipe
    ]
    my_slot = chip * n_pipe + z

    @pl.when(collects)
    def _():
        columns = []
        for start in range(0, tokens, 128):
            columns.append(
                jnp.broadcast_to(ids[:, start:start + 128].astype(jnp.float32), (128, 128)).T[:, :1]
            )
        column = jnp.concatenate(columns, axis=0)
        same = jnp.where(column == ids.astype(jnp.float32), 1.0, 0.0)
        here = lax.broadcasted_iota(jnp.int32, same.shape, 0)
        other = lax.broadcasted_iota(jnp.int32, same.shape, 1)
        earlier = jnp.sum(jnp.where(other < here, same, 0.0), axis=1, keepdims=True)
        first[...] = jnp.where(earlier == 0.0, same, 0.0).astype(jnp.bfloat16)
        with jax.named_scope("parts"):
            taken(gathered, part_sem.at[1])
        summed = jnp.dot(
            first[...], gathered[...].reshape(tokens, tile), preferred_element_type=jnp.float32
        )
        squares = jnp.sum(summed * summed, axis=0, keepdims=True)
        total = squares[:, :128]
        for lane in range(128, tile, 128):
            total = total + squares[:, lane:lane + 128]
        sums[my_slot] = total
        with jax.named_scope("line"):
            pl.semaphore_wait(line_sem, n_dp - 1)
        with jax.named_scope("share"):
            for ahead, up in targets:
                sum_copy(ahead, up, my_slot).start()

    for part in range(chunks):
        with jax.named_scope("relay"):
            arrived(1, part)
            copy(relayed, part, relay_to, 2).start()
            copy(relayed, part, sibling, 3).start()
            arrived(0, part)
            copy(relay_to, part, sibling, 3).start()

    vocab = made_ref.shape[0]
    wanted = lax.broadcasted_iota(jnp.int32, (vocab, tokens), 0) + me * vocab
    hot[...] = jnp.where(wanted == ids, 1.0, 0.0).astype(jnp.bfloat16)

    def forward(part):
        with jax.named_scope("diagonal"):
            arrived(2, part)
            copy(diagonal, part, sibling, 3).start()

    def make(part):
        with jax.named_scope("rest"):
            arrived(3, part, n_dp // 2)
        made_ref[:, part * tile:(part + 1) * tile] = jnp.dot(
            hot[...], held[part].reshape(tokens, tile), preferred_element_type=jnp.float32
        )

    forward(0)
    for part in range(1, chunks):
        forward(part)
        make(part - 1)
    make(chunks - 1)

    taken(held.at[:, pl.ds(0, n_dp - 1)], send_sem.at[0])
    taken(id_held.at[pl.ds(0, n_dp - 1)], id_sem.at[0])
    partials = chunks * n_pipe

    @pl.when(collects)
    def _():
        taken(gathered.at[pl.ds(0, chunks - 1)], part_sem.at[0])
        taken(sums.at[pl.ds(0, n_dp * n_pipe - 1)], sum_sem.at[0])
        with jax.named_scope("sums"):
            taken(sums.at[pl.ds(0, partials - 1)], sum_sem.at[1])

    @pl.when(jnp.logical_not(collects))
    def _():
        taken(gathered.at[pl.ds(0, chunks)], part_sem.at[0])
        with jax.named_scope("sums"):
            taken(sums.at[pl.ds(0, partials)], sum_sem.at[1])

    whole = sums[0]
    for slot in range(1, partials):
        whole = whole + sums[slot]
    norm = jnp.sqrt(jnp.sum(whole, axis=1, keepdims=True) * (scale * scale) + 1e-06)
    factor = jnp.minimum(1.0, clip / norm) * scale
    factor_ref[...] = jnp.broadcast_to(factor, factor_ref.shape)


def rows_kernel(factor_ref, made_ref, out_ref, scaled, sem):
    height = scaled.shape[0] // STRIPES
    factor = factor_ref[:, :1]
    for stripe in range(STRIPES):
        where = pl.ds(stripe * height, height)
        scaled[where] = made_ref[where] * factor
        pltpu.make_async_copy(scaled.at[where], out_ref.at[where], sem.at[0]).start()
    pltpu.make_async_copy(scaled, out_ref, sem.at[0]).wait()


def rows_of(made, factor):
    vmem = pl.BlockSpec(memory_space=pltpu.VMEM)
    return pl.pallas_call(
        rows_kernel,
        out_shape=jax.ShapeDtypeStruct(made.shape, jnp.float32),
        in_specs=[vmem, vmem],
        out_specs=pl.BlockSpec(memory_space=pltpu.HBM),
        scratch_shapes=[
            pltpu.VMEM(made.shape, jnp.float32),
            pltpu.SemaphoreType.DMA((1,)),
        ],
        compiler_params=pltpu.CompilerParams(vmem_limit_bytes=24 * 2**20),
        name="rows",
    )(factor, made)


def per_device(embed_grad, ids):
    n_dp, n_pipe = lax.axis_size("dp"), lax.axis_size("pipe")
    count, width = embed_grad.shape
    features = width * n_pipe
    tokens = count * n_dp
    tile = width // CHUNKS
    vmem = pl.BlockSpec(memory_space=pltpu.VMEM)
    hbm = pl.BlockSpec(memory_space=pltpu.HBM)
    made, factor = pl.pallas_call(
        functools.partial(
            gather_kernel, n_dp, n_pipe, 0.2 * math.sqrt(tokens * features), math.sqrt(features)
        ),
        out_shape=(
            pltpu.VMEM((VOC_DEV, width), jnp.float32),
            pltpu.VMEM((1, 128), jnp.float32),
        ),
        in_specs=[hbm, hbm],
        out_specs=(vmem, vmem),
        scratch_shapes=[
            pltpu.VMEM((CHUNKS, n_dp, count, tile), embed_grad.dtype),
            pltpu.VMEM((n_dp, 1, count), jnp.int32),
            pltpu.VMEM((n_dp, count, tile), embed_grad.dtype),
            pltpu.VMEM((tokens, tokens), jnp.bfloat16),
            pltpu.VMEM((VOC_DEV, tokens), jnp.bfloat16),
            pltpu.VMEM((n_dp * n_pipe, 1, 128), jnp.float32),
            pltpu.SemaphoreType.DMA((2,)),
            pltpu.SemaphoreType.REGULAR,
            pltpu.SemaphoreType.REGULAR,
            pltpu.SemaphoreType.REGULAR,
            pltpu.SemaphoreType.DMA((1,)),
            pltpu.SemaphoreType.DMA((4, CHUNKS)),
            pltpu.SemaphoreType.DMA((2,)),
            pltpu.SemaphoreType.DMA((2,)),
            pltpu.SemaphoreType.DMA((2,)),
        ],
        compiler_params=pltpu.CompilerParams(
            collective_id=0, has_side_effects=True, vmem_limit_bytes=32 * 2**20
        ),
        name="gather",
    )(
        pltpu.with_memory_space_constraint(embed_grad, pltpu.HBM),
        pltpu.with_memory_space_constraint(ids.reshape(1, count), pltpu.HBM),
    )
    return rows_of(made, factor)


def per_device_any(embed_grad, ids):
    tokens_all = embed_grad.shape[0] * lax.axis_size("dp")
    features = embed_grad.shape[1] * lax.axis_size("pipe")
    offset = lax.axis_index("dp") * VOC_DEV
    cotangent_all = lax.all_gather(embed_grad, "dp", axis=0, tiled=True)
    local = lax.all_gather(ids, "dp", axis=0, tiled=True) - offset
    inside = (local >= 0) & (local < VOC_DEV)
    segment = jnp.where(inside, local, VOC_DEV).astype(jnp.int32)
    summed = jax.ops.segment_sum(cotangent_all.astype(jnp.float32), segment, VOC_DEV + 1)
    grad_rows = summed[:VOC_DEV] * math.sqrt(features)
    total = lax.psum(jnp.sum(grad_rows * grad_rows), ("dp", "pipe"))
    grad_norm = jnp.sqrt(total + 1e-06)
    return grad_rows * jnp.minimum(1.0, 0.2 * math.sqrt(tokens_all * features) / grad_norm)


def solution(mesh):
    placed = (P("dp", "pipe"), P("dp"))
    cube = mesh.shape["dp"] == 2 * 2 * 2
    return jax.shard_map(
        per_device if cube else per_device_any, mesh=mesh, in_specs=placed,
        out_specs=P("dp", "pipe"), check_vma=False,
    )
```

time: 22.5 us -> 19.2 us (0.85)
  Pallas kernels: 22.3 us -> 19.1 us
    pallas_call x1, Pallas kernels: 19.1 us -> 16.2 us  [per_device(): pl.pallas_call(functools.partial(gather_kernel, n_dp, n_pipe, 0.2 * math....]
    pallas_call x1, Pallas kernels: 3.21 us -> 2.86 us  [rows_of(): pl.pallas_call(rows_kernel, out_shape=jax.ShapeDtypeStruct(made.shape, jn...]
where the time goes in v1:
time: 19.2 us; the launch traced here: 19.1 us
  Pallas kernels  19.1 us (99%)
    pallas_call x1, Pallas kernels, per_device(): pl.pallas_call(functools.partial(gather_kernel, n_dp, n_pipe, 0.2 * math....  16.2 us
    pallas_call x1, Pallas kernels, rows_of(): pl.pallas_call(rows_kernel, out_shape=jax.ShapeDtypeStruct(made.shape, jn...  2.86 us

profile of v1, /device:TPU:0, one launch (start us, length us, event | category | flops | bytes accessed | tf_op | source)
XLA Modules:
  0.0 19.1 jit_solution(15514602800247719)
XLA Ops:
  0.0 16.2 %gather.1 = (f32[1408,1152]{1,0:T(8,128)S(1)}, f32[1,128]{1,0:T(1,128)S(1)}) custom-call(bf16[64,1152]{1,0:T(8,128)(2,1)} %grad_ref.1, s32[1,64]{1,0:T(1,128)} %bitcast.1), custom_call_target="tpu_custom_call" | custom-call | tf_op jit(solution)/shard_map/gather/pallas_call | solution.py:282
  16.2 2.9 %rows.1 = f32[1408,1152]{1,0:T(8,128)} custom-call(f32[1,128]{1,0:T(1,128)S(1)} %get-tuple-element.7.factor_ref, f32[1408,1152]{1,0:T(8,128)S(1)} %get-tuple-element.8.made_ref), custom_call_target="tpu_custom_call" | custom-call | tf_op jit(solution)/shard_map/rows/pallas_call | solution.py:260

commit v2 on v1

--- a/solution.py
+++ b/solution.py
@@ -10,12 +10,28 @@
 
 VOC_DEV = 1408
 CHUNKS = 3
-STRIPES = 8
+STRIPES = 44
 MESH = pl.DeviceIdType.MESH
 
 
+def count_sends(device, n_dp, chunks):
+    chip, core = device // 2, device % 2
+    to_x, to_y = 2 - 4 * (chip % 2), 4 - 8 * (chip // 2)
+    relay_to, relayed = (device + to_x, device + to_y)[::1 if core else -1]
+    pieces = 0
+    for part in range(chunks):
+        pieces += device != 2 * part + 1
+        pieces += (relay_to // 2 != part) + (relayed // 2 != part)
+        pieces += chip != part or core == 1
+        if chip != part:
+            pieces += (relay_to // 2 != part) + 3
+        elif core == 1:
+            pieces += n_dp
+    return pieces
+
+
 def gather_kernel(n_dp, n_pipe, clip, scale, grad_ref, ids_ref, made_ref, factor_ref,
-                  held, id_held, gathered, first, hot, sums, load_sem, late_sem, far_sem, line_sem,
+                  held, id_held, first, hot, sums, load_sem, late_sem, far_sem, line_sem,
                   send_sem, recv_sem, id_sem, part_sem, sum_sem):
     me = lax.axis_index("dp")
     z = lax.axis_index("pipe")
@@ -27,7 +43,8 @@
     diagonal = me + to_x + to_y
     relayed = me + (1 - core) * to_x + core * to_y
     relay_to = me + core * to_x + (1 - core) * to_y
-    chunks, _, count, tile = held.shape
+    _, count, tile = held.shape
+    chunks = grad_ref.shape[1] // tile
     tokens = n_dp * count
     last_chip = n_dp // 2 - 1
     late = chip == last_chip
@@ -36,14 +53,14 @@
     def collector(part):
         return 2 * part + 1
 
+    def slot(part, block):
+        return part * n_dp + block
+
     load_ids = pltpu.make_async_copy(ids_ref, id_held.at[me], load_sem.at[0])
     load_ids.start()
     for part in range(chunks):
         columns = grad_ref.at[:, pl.ds(part * tile, tile)]
-        pltpu.make_async_copy(columns, held.at[part, me], load_sem.at[1]).start()
-        pl.when(me == collector(part))(
-            pltpu.make_async_copy(columns, gathered.at[me], part_sem.at[1]).start
-        )
+        pltpu.make_async_copy(columns, held.at[slot(part, me)], load_sem.at[1]).start()
 
     def taken(ref, semaphore):
         pltpu.make_async_copy(ref, ref, semaphore).wait()
@@ -90,32 +107,30 @@
         early = (lax.rem(me + ahead, n_dp) // 2 < last_chip) | late
         pl.when(early)(lambda ahead=ahead: id_copy(ahead).start())
 
-    def part_copy(part):
+    def copy_by(block, part, target, semaphore):
         return pltpu.make_async_remote_copy(
-            src_ref=held.at[part, me], dst_ref=gathered.at[me],
-            send_sem=part_sem.at[0], recv_sem=part_sem.at[1],
-            device_id=(collector(part), z), device_id_type=MESH,
-        )
-
-    taken(held.at[:, me], load_sem.at[1])
-    for part in range(chunks):
-        pl.when(me != collector(part))(lambda part=part: part_copy(part).start())
+            src_ref=held.at[slot(part, block)], dst_ref=held.at[slot(part, block)],
+            send_sem=send_sem.at[0], recv_sem=semaphore,
+            device_id=(target, z), device_id_type=MESH,
+        )
 
     def copy(block, part, target, place):
-        return pltpu.make_async_remote_copy(
-            src_ref=held.at[part, block], dst_ref=held.at[part, block],
-            send_sem=send_sem.at[0], recv_sem=recv_sem.at[place, part],
-            device_id=(target, z), device_id_type=MESH,
-        )
-
-    def arrived(place, part, count=1):
-        taken(held.at[part, pl.ds(0, count)], recv_sem.at[place, part])
+        return copy_by(block, part, target, recv_sem.at[place, part])
+
+    def arrived(place, part, pieces=1):
+        taken(held.at[pl.ds(0, pieces)], recv_sem.at[place, part])
+
+    taken(held.at[pl.ds(0, chunks)], load_sem.at[1])
+    for part in range(chunks):
+        pl.when(me != collector(part))(copy_by(me, part, collector(part), part_sem.at[0]).start)
 
     own = [(relay_to, 0), (relayed, 1)]
 
     def send_own(part):
         for target, place in own:
-            pl.when(late | (target // 2 < last_chip))(copy(me, part, target, place).start)
+            pl.when((target // 2 != part) & (late | (target // 2 < last_chip)))(
+                copy(me, part, target, place).start
+            )
 
     def send_late(part):
         for target, place in own:
@@ -135,7 +150,7 @@
         send_own(part)
         pl.when(chip < last_chip)(lambda part=part: send_late(part))
     for part in range(chunks):
-        copy(me, part, sibling, 3).start()
+        pl.when((chip != part) | (core == 1))(copy(me, part, sibling, 3).start)
 
     with jax.named_scope("far"):
         @pl.when(z < n_pipe - 1)
@@ -148,9 +163,9 @@
         taken(id_held.at[pl.ds(0, n_dp - 1)], id_sem.at[1])
     ids = jnp.concatenate([id_held[block] for block in range(n_dp)], axis=1)
 
-    def sum_copy(ahead, up, slot):
+    def sum_copy(ahead, up, share):
         return pltpu.make_async_remote_copy(
-            src_ref=sums.at[slot], dst_ref=sums.at[slot],
+            src_ref=sums.at[share], dst_ref=sums.at[share],
             send_sem=sum_sem.at[0], recv_sem=sum_sem.at[1],
             device_id=(lax.rem(me + ahead, n_dp), lax.rem(z + up, n_pipe)), device_id_type=MESH,
         )
@@ -175,9 +190,10 @@
         earlier = jnp.sum(jnp.where(other < here, same, 0.0), axis=1, keepdims=True)
         first[...] = jnp.where(earlier == 0.0, same, 0.0).astype(jnp.bfloat16)
         with jax.named_scope("parts"):
-            taken(gathered, part_sem.at[1])
+            taken(held.at[pl.ds(0, n_dp - 1)], part_sem.at[0])
         summed = jnp.dot(
-            first[...], gathered[...].reshape(tokens, tile), preferred_element_type=jnp.float32
+            first[...], held[pl.ds(chip * n_dp, n_dp)].reshape(tokens, tile),
+            preferred_element_type=jnp.float32,
         )
         squares = jnp.sum(summed * summed, axis=0, keepdims=True)
         total = squares[:, :128]
@@ -190,50 +206,79 @@
             for ahead, up in targets:
                 sum_copy(ahead, up, my_slot).start()
 
-    for part in range(chunks):
-        with jax.named_scope("relay"):
-            arrived(1, part)
-            copy(relayed, part, relay_to, 2).start()
-            copy(relayed, part, sibling, 3).start()
-            arrived(0, part)
-            copy(relay_to, part, sibling, 3).start()
+        copy(sibling + to_x, chip, sibling + to_y, 2).start()
+        copy(relayed, chip, relay_to, 2).start()
+        for block in (me + to_x, me + to_y, diagonal):
+            copy(block, chip, sibling, 3).start()
+        for block, place in ((to_y, 0), (to_x, 1), (to_x + to_y, 2)):
+            copy(sibling + block, chip, sibling, place).start()
+
+    for part in range(chunks):
+        @pl.when(chip != part)
+        def _():
+            with jax.named_scope("relay"):
+                arrived(1, part)
+                pl.when(relay_to // 2 != part)(copy(relayed, part, relay_to, 2).start)
+                copy(relayed, part, sibling, 3).start()
+                arrived(0, part)
+                copy(relay_to, part, sibling, 3).start()
 
     vocab = made_ref.shape[0]
     wanted = lax.broadcasted_iota(jnp.int32, (vocab, tokens), 0) + me * vocab
     hot[...] = jnp.where(wanted == ids, 1.0, 0.0).astype(jnp.bfloat16)
 
     def forward(part):
-        with jax.named_scope("diagonal"):
-            arrived(2, part)
-            copy(diagonal, part, sibling, 3).start()
-
-    def make(part):
+        @pl.when(chip != part)
+        def _():
+            with jax.named_scope("diagonal"):
+                arrived(2, part)
+                copy(diagonal, part, sibling, 3).start()
+
+    def make(part, start, stop):
         with jax.named_scope("rest"):
-            arrived(3, part, n_dp // 2)
-        made_ref[:, part * tile:(part + 1) * tile] = jnp.dot(
-            hot[...], held[part].reshape(tokens, tile), preferred_element_type=jnp.float32
+            @pl.when((chip == part) & (core == 0))
+            def _():
+                for place in range(3):
+                    arrived(place, part)
+
+            pl.when((chip != part) | (core == 0))(lambda: arrived(3, part, n_dp // 2))
+        pieces = []
+        for index in range(start // tile, part + 1):
+            block = held[pl.ds(index * n_dp, n_dp)].reshape(tokens, tile)
+            low, high = max(start - index * tile, 0), min(stop - index * tile, tile)
+            pieces.append(block[:, low:high])
+        made_ref[:, start:stop] = jnp.dot(
+            hot[...], jnp.concatenate(pieces, axis=1), preferred_element_type=jnp.float32
         )
 
     forward(0)
-    for part in range(1, chunks):
-        forward(part)
-        make(part - 1)
-    make(chunks - 1)
-
-    taken(held.at[:, pl.ds(0, n_dp - 1)], send_sem.at[0])
+    done = 0
+    for part in range(chunks):
+        if part < chunks - 1:
+            forward(part + 1)
+        stop = (part + 1) * tile
+        if part < chunks - 1:
+            stop -= stop % 256
+        make(part, done, stop)
+        done = stop
+
+    counts = [count_sends(device, n_dp, chunks) for device in range(n_dp)]
+    for pieces in sorted(set(counts)):
+        mine = functools.reduce(
+            jnp.logical_or, [me == device for device in range(n_dp) if counts[device] == pieces]
+        )
+        pl.when(mine)(lambda pieces=pieces: taken(held.at[pl.ds(0, pieces)], send_sem.at[0]))
     taken(id_held.at[pl.ds(0, n_dp - 1)], id_sem.at[0])
     partials = chunks * n_pipe
 
     @pl.when(collects)
     def _():
-        taken(gathered.at[pl.ds(0, chunks - 1)], part_sem.at[0])
         taken(sums.at[pl.ds(0, n_dp * n_pipe - 1)], sum_sem.at[0])
         with jax.named_scope("sums"):
             taken(sums.at[pl.ds(0, partials - 1)], sum_sem.at[1])
 
     @pl.when(jnp.logical_not(collects))
     def _():
-        taken(gathered.at[pl.ds(0, chunks)], part_sem.at[0])
         with jax.named_scope("sums"):
             taken(sums.at[pl.ds(0, partials)], sum_sem.at[1])
 
@@ -290,9 +335,8 @@
         in_specs=[hbm, hbm],
         out_specs=(vmem, vmem),
         scratch_shapes=[
-            pltpu.VMEM((CHUNKS, n_dp, count, tile), embed_grad.dtype),
+            pltpu.VMEM((CHUNKS * n_dp + 4, count, tile), embed_grad.dtype),
             pltpu.VMEM((n_dp, 1, count), jnp.int32),
-            pltpu.VMEM((n_dp, count, tile), embed_grad.dtype),
             pltpu.VMEM((tokens, tokens), jnp.bfloat16),
             pltpu.VMEM((VOC_DEV, tokens), jnp.bfloat16),
             pltpu.VMEM((n_dp * n_pipe, 1, 128), jnp.float32),
@@ -303,7 +347,7 @@
             pltpu.SemaphoreType.DMA((1,)),
             pltpu.SemaphoreType.DMA((4, CHUNKS)),
             pltpu.SemaphoreType.DMA((2,)),
-            pltpu.SemaphoreType.DMA((2,)),
+            pltpu.SemaphoreType.DMA((1,)),
             pltpu.SemaphoreType.DMA((2,)),
         ],
         compiler_params=pltpu.CompilerParams(

time: 19.2 us -> 18.1 us (0.943)
  Pallas kernels: 19.1 us -> 17.8 us
    pallas_call x1, Pallas kernels: 16.2 us -> 15 us  [per_device(): pl.pallas_call(functools.partial(gather_kernel, n_dp, n_pipe, 0.2 * math....]
where the time goes in v2:
time: 18.1 us; the launch traced here: 17.8 us
  Pallas kernels  17.8 us (98%)
    pallas_call x1, Pallas kernels, per_device(): pl.pallas_call(functools.partial(gather_kernel, n_dp, n_pipe, 0.2 * math....  15 us
    pallas_call x1, Pallas kernels, rows_of(): pl.pallas_call(rows_kernel, out_shape=jax.ShapeDtypeStruct(made.shape, jn...  2.77 us

profile of v2, /device:TPU:0, one launch (start us, length us, event | category | flops | bytes accessed | tf_op | source)
XLA Modules:
  0.0 17.8 jit_solution(10689425424273903899)
XLA Ops:
  0.0 15.0 %gather.1 = (f32[1408,1152]{1,0:T(8,128)S(1)}, f32[1,128]{1,0:T(1,128)S(1)}) custom-call(bf16[64,1152]{1,0:T(8,128)(2,1)} %grad_ref.1, s32[1,64]{1,0:T(1,128)} %bitcast.1), custom_call_target="tpu_custom_call" | custom-call | tf_op jit(solution)/shard_map/gather/pallas_call | solution.py:327
  15.0 2.8 %rows.1 = f32[1408,1152]{1,0:T(8,128)} custom-call(f32[1,128]{1,0:T(1,128)S(1)} %get-tuple-element.7.factor_ref, f32[1408,1152]{1,0:T(8,128)S(1)} %get-tuple-element.8.made_ref), custom_call_target="tpu_custom_call" | custom-call | tf_op jit(solution)/shard_map/rows/pallas_call | solution.py:305

commit v3 on v2

--- a/solution.py
+++ b/solution.py
@@ -31,7 +31,7 @@
 
 
 def gather_kernel(n_dp, n_pipe, clip, scale, grad_ref, ids_ref, made_ref, factor_ref,
-                  held, id_held, first, hot, sums, load_sem, late_sem, far_sem, line_sem,
+                  held, id_held, first, hot, sums, load_sem, cross_sem, late_sem, far_sem, line_sem,
                   send_sem, recv_sem, id_sem, part_sem, sum_sem):
     me = lax.axis_index("dp")
     z = lax.axis_index("pipe")
@@ -72,18 +72,35 @@
 
     greet(barrier, sibling, z)
 
-    @pl.when(chip < last_chip)
+    leads = chip == 0
+    between = jnp.logical_not(leads | late)
+
+    def apart(target):
+        return (chip + target // 2 == last_chip) & between
+
+    @pl.when(jnp.logical_not(late))
     def _():
         for ahead in range(2, n_dp, 2):
-            for other in range(2):
-                greet(barrier, lax.rem(2 * chip + ahead, n_dp) + other, z)
+            target = lax.rem(2 * chip + ahead, n_dp)
+
+            @pl.when(jnp.logical_not(apart(target)))
+            def _():
+                for other in range(2):
+                    greet(barrier, target + other, z)
 
     for other in range(1, n_pipe):
         @pl.when(z < other)
         def _():
             greet(barrier, me, other)
     with jax.named_scope("barrier"):
-        pl.semaphore_wait(barrier, jnp.where(late, n_dp - 1, n_dp - 3) + z)
+        near = jnp.where(leads, n_dp - 3, jnp.where(late, n_dp - 1, 3))
+        pl.semaphore_wait(barrier, near + z)
+
+    @pl.when(me == 1)
+    def _():
+        for target in range(2, n_dp - 2):
+            greet(cross_sem, target, z)
+
     load_ids.wait()
 
     @pl.when(late)
@@ -104,7 +121,8 @@
         )
 
     for ahead in range(1, n_dp):
-        early = (lax.rem(me + ahead, n_dp) // 2 < last_chip) | late
+        target = lax.rem(me + ahead, n_dp)
+        early = ((target // 2 < last_chip) | late) & jnp.logical_not(apart(target))
         pl.when(early)(lambda ahead=ahead: id_copy(ahead).start())
 
     def copy_by(block, part, target, semaphore):
@@ -120,9 +138,14 @@
     def arrived(place, part, pieces=1):
         taken(held.at[pl.ds(0, pieces)], recv_sem.at[place, part])
 
+    order = [*range(1, chunks), 0]
     taken(held.at[pl.ds(0, chunks)], load_sem.at[1])
-    for part in range(chunks):
-        pl.when(me != collector(part))(copy_by(me, part, collector(part), part_sem.at[0]).start)
+    hurried = late & (core == 0) & (z == 0)
+    pl.when(hurried)(copy(me, 1, relayed, 1).start)
+    for part in order:
+        pl.when((me != collector(part)) & jnp.logical_not(apart(collector(part))))(
+            copy_by(me, part, collector(part), part_sem.at[0]).start
+        )
 
     own = [(relay_to, 0), (relayed, 1)]
 
@@ -136,7 +159,22 @@
         for target, place in own:
             pl.when(target // 2 == last_chip)(copy(me, part, target, place).start)
 
-    send_own(0)
+    for target, place in own:
+        pl.when((target // 2 != 1) & (late | (target // 2 < last_chip)) & jnp.logical_not(hurried))(
+            copy(me, 1, target, place).start
+        )
+    with jax.named_scope("cross"):
+        @pl.when(between)
+        def _():
+            pl.semaphore_wait(cross_sem, 1)
+            for ahead in range(1, n_dp):
+                pl.when(apart(lax.rem(me + ahead, n_dp)))(
+                    lambda ahead=ahead: id_copy(ahead).start()
+                )
+            for part in range(1, chunks):
+                pl.when(apart(collector(part)))(
+                    copy_by(me, part, collector(part), part_sem.at[0]).start
+                )
     with jax.named_scope("late"):
         @pl.when(chip < last_chip)
         def _():
@@ -145,11 +183,11 @@
                 pl.when(lax.rem(me + ahead, n_dp) // 2 == last_chip)(
                     lambda ahead=ahead: id_copy(ahead).start()
                 )
-            send_late(0)
-    for part in range(1, chunks):
+            send_late(1)
+    for part in order[1:]:
         send_own(part)
         pl.when(chip < last_chip)(lambda part=part: send_late(part))
-    for part in range(chunks):
+    for part in order:
         pl.when((chip != part) | (core == 1))(copy(me, part, sibling, 3).start)
 
     with jax.named_scope("far"):
@@ -213,7 +251,7 @@
         for block, place in ((to_y, 0), (to_x, 1), (to_x + to_y, 2)):
             copy(sibling + block, chip, sibling, place).start()
 
-    for part in range(chunks):
+    for part in order:
         @pl.when(chip != part)
         def _():
             with jax.named_scope("relay"):
@@ -243,7 +281,7 @@
 
             pl.when((chip != part) | (core == 0))(lambda: arrived(3, part, n_dp // 2))
         pieces = []
-        for index in range(start // tile, part + 1):
+        for index in range(start // tile, -(-stop // tile)):
             block = held[pl.ds(index * n_dp, n_dp)].reshape(tokens, tile)
             low, high = max(start - index * tile, 0), min(stop - index * tile, tile)
             pieces.append(block[:, low:high])
@@ -251,16 +289,19 @@
             hot[...], jnp.concatenate(pieces, axis=1), preferred_element_type=jnp.float32
         )
 
-    forward(0)
-    done = 0
-    for part in range(chunks):
-        if part < chunks - 1:
-            forward(part + 1)
-        stop = (part + 1) * tile
-        if part < chunks - 1:
-            stop -= stop % 256
-        make(part, done, stop)
-        done = stop
+    def make_all(order, edges):
+        forward(order[0])
+        for place, part in enumerate(order):
+            if place < chunks - 1:
+                forward(order[place + 1])
+            make(part, *edges[part])
+
+    down = [part * tile - part * tile % 256 for part in range(chunks)] + [chunks * tile]
+    edges = [(down[part], down[part + 1]) for part in range(chunks)]
+    up = -(-tile // 256) * 256
+    pl.when(leads)(lambda: make_all(range(chunks), edges))
+    edges = [(0, up), (up, edges[1][1])] + edges[2:]
+    pl.when(jnp.logical_not(leads))(lambda: make_all(order, edges))
 
     counts = [count_sends(device, n_dp, chunks) for device in range(n_dp)]
     for pieces in sorted(set(counts)):
@@ -344,6 +385,7 @@
             pltpu.SemaphoreType.REGULAR,
             pltpu.SemaphoreType.REGULAR,
             pltpu.SemaphoreType.REGULAR,
+            pltpu.SemaphoreType.REGULAR,
             pltpu.SemaphoreType.DMA((1,)),
             pltpu.SemaphoreType.DMA((4, CHUNKS)),
             pltpu.SemaphoreType.DMA((2,)),

time: 18.1 us -> 17.2 us (0.950)
  Pallas kernels: 17.8 us -> 17.1 us
    pallas_call x1, Pallas kernels: 15 us -> 14.3 us  [per_device(): pl.pallas_call(functools.partial(gather_kernel, n_dp, n_pipe, 0.2 * math....]
where the time goes in v3:
time: 17.2 us; the launch traced here: 17.1 us
  Pallas kernels  17.1 us (99%)
    pallas_call x1, Pallas kernels, per_device(): pl.pallas_call(functools.partial(gather_kernel, n_dp, n_pipe, 0.2 * math....  14.3 us
    pallas_call x1, Pallas kernels, rows_of(): pl.pallas_call(rows_kernel, out_shape=jax.ShapeDtypeStruct(made.shape, jn...  2.77 us

profile of v3, /device:TPU:0, one launch (start us, length us, event | category | flops | bytes accessed | tf_op | source)
XLA Modules:
  0.0 17.1 jit_solution(7568440742331584571)
XLA Ops:
  0.0 14.3 %gather.1 = (f32[1408,1152]{1,0:T(8,128)S(1)}, f32[1,128]{1,0:T(1,128)S(1)}) custom-call(bf16[64,1152]{1,0:T(8,128)(2,1)} %grad_ref.1, s32[1,64]{1,0:T(1,128)} %bitcast.1), custom_call_target="tpu_custom_call" | custom-call | tf_op jit(solution)/shard_map/gather/pallas_call | solution.py:368
  14.3 2.8 %rows.1 = f32[1408,1152]{1,0:T(8,128)} custom-call(f32[1,128]{1,0:T(1,128)S(1)} %get-tuple-element.7.factor_ref, f32[1408,1152]{1,0:T(8,128)S(1)} %get-tuple-element.8.made_ref), custom_call_target="tpu_custom_call" | custom-call | tf_op jit(solution)/shard_map/rows/pallas_call | solution.py:346

commit v4 on v3

--- a/solution.py
+++ b/solution.py
@@ -31,7 +31,7 @@
 
 
 def gather_kernel(n_dp, n_pipe, clip, scale, grad_ref, ids_ref, made_ref, factor_ref,
-                  held, id_held, first, hot, sums, load_sem, cross_sem, late_sem, far_sem, line_sem,
+                  held, id_held, first, begun, hot, sums, load_sem, cross_sem, late_sem, far_sem, line_sem,
                   send_sem, recv_sem, id_sem, part_sem, sum_sem):
     me = lax.axis_index("dp")
     z = lax.axis_index("pipe")
@@ -50,6 +50,8 @@
     late = chip == last_chip
     collects = (core == 1) & (chip < chunks)
 
+    half = n_dp // 2
+
     def collector(part):
         return 2 * part + 1
 
@@ -144,7 +146,7 @@
     pl.when(hurried)(copy(me, 1, relayed, 1).start)
     for part in order:
         pl.when((me != collector(part)) & jnp.logical_not(apart(collector(part))))(
-            copy_by(me, part, collector(part), part_sem.at[0]).start
+            copy_by(me, part, collector(part), part_sem.at[me // half]).start
         )
 
     own = [(relay_to, 0), (relayed, 1)]
@@ -159,10 +161,15 @@
         for target, place in own:
             pl.when(target // 2 == last_chip)(copy(me, part, target, place).start)
 
-    for target, place in own:
-        pl.when((target // 2 != 1) & (late | (target // 2 < last_chip)) & jnp.logical_not(hurried))(
-            copy(me, 1, target, place).start
-        )
+    behind = between & (z > 0)
+
+    def send_first(when):
+        for target, place in own:
+            pl.when((target // 2 != 1) & (late | (target // 2 < last_chip)) & when)(
+                copy(me, 1, target, place).start
+            )
+
+    send_first(jnp.logical_not(hurried | behind))
     with jax.named_scope("cross"):
         @pl.when(between)
         def _():
@@ -173,8 +180,9 @@
                 )
             for part in range(1, chunks):
                 pl.when(apart(collector(part)))(
-                    copy_by(me, part, collector(part), part_sem.at[0]).start
+                    copy_by(me, part, collector(part), part_sem.at[me // half]).start
                 )
+    send_first(behind)
     with jax.named_scope("late"):
         @pl.when(chip < last_chip)
         def _():
@@ -188,7 +196,7 @@
         send_own(part)
         pl.when(chip < last_chip)(lambda part=part: send_late(part))
     for part in order:
-        pl.when((chip != part) | (core == 1))(copy(me, part, sibling, 3).start)
+        pl.when((chip != part) | (core == 1))(copy(me, part, sibling, 4).start)
 
     with jax.named_scope("far"):
         @pl.when(z < n_pipe - 1)
@@ -227,12 +235,26 @@
         other = lax.broadcasted_iota(jnp.int32, same.shape, 1)
         earlier = jnp.sum(jnp.where(other < here, same, 0.0), axis=1, keepdims=True)
         first[...] = jnp.where(earlier == 0.0, same, 0.0).astype(jnp.bfloat16)
-        with jax.named_scope("parts"):
-            taken(held.at[pl.ds(0, n_dp - 1)], part_sem.at[0])
-        summed = jnp.dot(
-            first[...], held[pl.ds(chip * n_dp, n_dp)].reshape(tokens, tile),
-            preferred_element_type=jnp.float32,
-        )
+        def summed_of(index):
+            with jax.named_scope("parts"):
+                mine = me // half == index
+                for own in (0, 1):
+                    pl.when(mine == (own == 1))(
+                        lambda: taken(held.at[pl.ds(0, half - own)], part_sem.at[index])
+                    )
+            if index == 1:
+                for block in (me + to_x, me + to_y, diagonal):
+                    copy(block, chip, sibling, 3).start()
+                for block, place in ((to_y, 0), (to_x, 1), (to_x + to_y, 2)):
+                    copy(sibling + block, chip, sibling, place).start()
+            return jnp.dot(
+                first[:, index * half * count:(index + 1) * half * count],
+                held[pl.ds(chip * n_dp + index * half, half)].reshape(half * count, tile),
+                preferred_element_type=jnp.float32,
+            )
+
+        begun[...] = summed_of(0)
+        summed = begun[...] + summed_of(1)
         squares = jnp.sum(summed * summed, axis=0, keepdims=True)
         total = squares[:, :128]
         for lane in range(128, tile, 128):
@@ -246,10 +268,6 @@
 
         copy(sibling + to_x, chip, sibling + to_y, 2).start()
         copy(relayed, chip, relay_to, 2).start()
-        for block in (me + to_x, me + to_y, diagonal):
-            copy(block, chip, sibling, 3).start()
-        for block, place in ((to_y, 0), (to_x, 1), (to_x + to_y, 2)):
-            copy(sibling + block, chip, sibling, place).start()
 
     for part in order:
         @pl.when(chip != part)
@@ -262,8 +280,33 @@
                 copy(relay_to, part, sibling, 3).start()
 
     vocab = made_ref.shape[0]
+    near_blocks = (me, sibling, relayed, relay_to)
+    far_blocks = (sibling + to_x, sibling + to_y, diagonal, sibling + to_x + to_y)
+    mixed = jnp.concatenate([id_held[block] for block in near_blocks + far_blocks], axis=1)
     wanted = lax.broadcasted_iota(jnp.int32, (vocab, tokens), 0) + me * vocab
-    hot[...] = jnp.where(wanted == ids, 1.0, 0.0).astype(jnp.bfloat16)
+    hot[...] = jnp.where(wanted == mixed, 1.0, 0.0).astype(jnp.bfloat16)
+
+    def stacked(blocks, start, stop):
+        pieces = []
+        for part in range(start // tile, -(-stop // tile)):
+            low, high = max(start - part * tile, 0), min(stop - part * tile, tile)
+            pieces.append(jnp.concatenate(
+                [held[slot(part, block)][:, low:high] for block in blocks], axis=0
+            ))
+        return jnp.concatenate(pieces, axis=1)
+
+    with jax.named_scope("near"):
+        for part in range(chunks):
+            @pl.when((chip == part) & (core == 0))
+            def _():
+                arrived(0, part)
+                arrived(1, part)
+
+            pl.when((chip != part) | (core == 0))(lambda part=part: arrived(4, part))
+    made_ref[...] = jnp.dot(
+        hot[:, :tokens // 2], stacked(near_blocks, 0, chunks * tile),
+        preferred_element_type=jnp.float32,
+    )
 
     def forward(part):
         @pl.when(chip != part)
@@ -274,19 +317,11 @@
 
     def make(part, start, stop):
         with jax.named_scope("rest"):
-            @pl.when((chip == part) & (core == 0))
-            def _():
-                for place in range(3):
-                    arrived(place, part)
-
-            pl.when((chip != part) | (core == 0))(lambda: arrived(3, part, n_dp // 2))
-        pieces = []
-        for index in range(start // tile, -(-stop // tile)):
-            block = held[pl.ds(index * n_dp, n_dp)].reshape(tokens, tile)
-            low, high = max(start - index * tile, 0), min(stop - index * tile, tile)
-            pieces.append(block[:, low:high])
-        made_ref[:, start:stop] = jnp.dot(
-            hot[...], jnp.concatenate(pieces, axis=1), preferred_element_type=jnp.float32
+            pl.when((chip == part) & (core == 0))(lambda: arrived(2, part))
+            pl.when((chip != part) | (core == 0))(lambda: arrived(3, part, n_dp // 2 - 1))
+        made_ref[:, start:stop] += jnp.dot(
+            hot[:, tokens // 2:], stacked(far_blocks, start, stop),
+            preferred_element_type=jnp.float32,
         )
 
     def make_all(order, edges):
@@ -379,6 +414,7 @@
             pltpu.VMEM((CHUNKS * n_dp + 4, count, tile), embed_grad.dtype),
             pltpu.VMEM((n_dp, 1, count), jnp.int32),
             pltpu.VMEM((tokens, tokens), jnp.bfloat16),
+            pltpu.VMEM((tokens, tile), jnp.float32),
             pltpu.VMEM((VOC_DEV, tokens), jnp.bfloat16),
             pltpu.VMEM((n_dp * n_pipe, 1, 128), jnp.float32),
             pltpu.SemaphoreType.DMA((2,)),
@@ -387,9 +423,9 @@
             pltpu.SemaphoreType.REGULAR,
             pltpu.SemaphoreType.REGULAR,
             pltpu.SemaphoreType.DMA((1,)),
-            pltpu.SemaphoreType.DMA((4, CHUNKS)),
+            pltpu.SemaphoreType.DMA((5, CHUNKS)),
             pltpu.SemaphoreType.DMA((2,)),
-            pltpu.SemaphoreType.DMA((1,)),
+            pltpu.SemaphoreType.DMA((2,)),
             pltpu.SemaphoreType.DMA((2,)),
         ],
         compiler_params=pltpu.CompilerParams(

time: 17.2 us -> 16.6 us (0.965)
  Pallas kernels: 17.1 us -> 16.5 us
    pallas_call x1, Pallas kernels: 14.3 us -> 13.7 us  [per_device(): pl.pallas_call(functools.partial(gather_kernel, n_dp, n_pipe, 0.2 * math....]
where the time goes in v4:
time: 16.6 us; the launch traced here: 16.5 us
  Pallas kernels  16.5 us (99%)
    pallas_call x1, Pallas kernels, per_device(): pl.pallas_call(functools.partial(gather_kernel, n_dp, n_pipe, 0.2 * math....  13.7 us
    pallas_call x1, Pallas kernels, rows_of(): pl.pallas_call(rows_kernel, out_shape=jax.ShapeDtypeStruct(made.shape, jn...  2.77 us

profile of v4, /device:TPU:0, one launch (start us, length us, event | category | flops | bytes accessed | tf_op | source)
XLA Modules:
  0.0 16.5 jit_solution(423775608095048219)
XLA Ops:
  0.0 13.7 %gather.1 = (f32[1408,1152]{1,0:T(8,128)S(1)}, f32[1,128]{1,0:T(1,128)S(1)}) custom-call(bf16[64,1152]{1,0:T(8,128)(2,1)} %grad_ref.1, s32[1,64]{1,0:T(1,128)} %bitcast.1), custom_call_target="tpu_custom_call" | custom-call | tf_op jit(solution)/shard_map/gather/pallas_call | solution.py:403
  13.7 2.8 %rows.1 = f32[1408,1152]{1,0:T(8,128)} custom-call(f32[1,128]{1,0:T(1,128)S(1)} %get-tuple-element.7.factor_ref, f32[1408,1152]{1,0:T(8,128)S(1)} %get-tuple-element.8.made_ref), custom_call_target="tpu_custom_call" | custom-call | tf_op jit(solution)/shard_map/rows/pallas_call | solution.py:381

commit v5 on v4

--- a/solution.py
+++ b/solution.py
@@ -32,7 +32,7 @@
 
 def gather_kernel(n_dp, n_pipe, clip, scale, grad_ref, ids_ref, made_ref, factor_ref,
                   held, id_held, first, begun, hot, sums, load_sem, cross_sem, late_sem, far_sem, line_sem,
-                  send_sem, recv_sem, id_sem, part_sem, sum_sem):
+                  send_sem, recv_sem, twin_sem, id_sem, part_sem, sum_sem):
     me = lax.axis_index("dp")
     z = lax.axis_index("pipe")
     chip, core = me // 2, lax.rem(me, 2)
@@ -75,7 +75,7 @@
     greet(barrier, sibling, z)
 
     leads = chip == 0
-    between = jnp.logical_not(leads | late)
+    between = jnp.logical_not(leads | late) & ((z == 0) | (chip == 1))
 
     def apart(target):
         return (chip + target // 2 == last_chip) & between
@@ -85,7 +85,9 @@
         for ahead in range(2, n_dp, 2):
             target = lax.rem(2 * chip + ahead, n_dp)
 
-            @pl.when(jnp.logical_not(apart(target)))
+            opposite = (chip + target // 2 == last_chip) & jnp.logical_not(leads)
+
+            @pl.when(jnp.logical_not(opposite) | ((chip == 1) & (z > 0)))
             def _():
                 for other in range(2):
                     greet(barrier, target + other, z)
@@ -95,13 +97,13 @@
         def _():
             greet(barrier, me, other)
     with jax.named_scope("barrier"):
-        near = jnp.where(leads, n_dp - 3, jnp.where(late, n_dp - 1, 3))
+        near = jnp.where(between, 3, jnp.where(late, n_dp - 1, n_dp - 3))
         pl.semaphore_wait(barrier, near + z)
 
     @pl.when(me == 1)
     def _():
         for target in range(2, n_dp - 2):
-            greet(cross_sem, target, z)
+            pl.when((z == 0) | (target // 2 == 1))(lambda target=target: greet(cross_sem, target, z))
 
     load_ids.wait()
 
@@ -144,10 +146,16 @@
     taken(held.at[pl.ds(0, chunks)], load_sem.at[1])
     hurried = late & (core == 0) & (z == 0)
     pl.when(hurried)(copy(me, 1, relayed, 1).start)
+    upper = late & (z > 0)
+
+    def send_part(part, when):
+        pl.when((me != collector(part)) & jnp.logical_not(apart(collector(part))) & when)(
+            copy_by(me, part, collector(part), part_sem.at[me // half]).start
+        )
+
+    send_part(0, upper)
     for part in order:
-        pl.when((me != collector(part)) & jnp.logical_not(apart(collector(part))))(
-            copy_by(me, part, collector(part), part_sem.at[me // half]).start
-        )
+        send_part(part, jnp.logical_not(upper) if part == 0 else True)
 
     own = [(relay_to, 0), (relayed, 1)]
 
@@ -196,7 +204,7 @@
         send_own(part)
         pl.when(chip < last_chip)(lambda part=part: send_late(part))
     for part in order:
-        pl.when((chip != part) | (core == 1))(copy(me, part, sibling, 4).start)
+        pl.when((chip != part) | (core == 1))(copy_by(me, part, sibling, twin_sem.at[0]).start)
 
     with jax.named_scope("far"):
         @pl.when(z < n_pipe - 1)
@@ -295,18 +303,23 @@
             ))
         return jnp.concatenate(pieces, axis=1)
 
-    with jax.named_scope("near"):
-        for part in range(chunks):
-            @pl.when((chip == part) & (core == 0))
-            def _():
-                arrived(0, part)
-                arrived(1, part)
-
-            pl.when((chip != part) | (core == 0))(lambda part=part: arrived(4, part))
-    made_ref[...] = jnp.dot(
-        hot[:, :tokens // 2], stacked(near_blocks, 0, chunks * tile),
-        preferred_element_type=jnp.float32,
-    )
+    def make_near(parts, start, stop):
+        with jax.named_scope("near"):
+            for part in parts:
+                @pl.when((chip == part) & (core == 0))
+                def _():
+                    arrived(0, part)
+                    arrived(1, part)
+        made_ref[:, start:stop] = jnp.dot(
+            hot[:, :tokens // 2], stacked(near_blocks, start, stop),
+            preferred_element_type=jnp.float32,
+        )
+
+    up = -(-tile // 256) * 256
+    pl.when(collects)(lambda: taken(held.at[pl.ds(0, chunks - 1)], twin_sem.at[0]))
+    pl.when(jnp.logical_not(collects))(lambda: taken(held.at[pl.ds(0, chunks)], twin_sem.at[0]))
+    make_near(order[:-1], up, chunks * tile)
+    make_near(order[-1:], 0, up)
 
     def forward(part):
         @pl.when(chip != part)
@@ -324,19 +337,33 @@
             preferred_element_type=jnp.float32,
         )
 
-    def make_all(order, edges):
-        forward(order[0])
-        for place, part in enumerate(order):
-            if place < chunks - 1:
-                forward(order[place + 1])
+    def make_all(order, edges, ahead):
+        for part in order[:1] if ahead else ():
+            make(part, *edges[part])
+        for part in order:
+            forward(part)
+        for part in order[1:] if ahead else order:
             make(part, *edges[part])
 
     down = [part * tile - part * tile % 256 for part in range(chunks)] + [chunks * tile]
     edges = [(down[part], down[part + 1]) for part in range(chunks)]
-    up = -(-tile // 256) * 256
-    pl.when(leads)(lambda: make_all(range(chunks), edges))
-    edges = [(0, up), (up, edges[1][1])] + edges[2:]
-    pl.when(jnp.logical_not(leads))(lambda: make_all(order, edges))
+
+    @pl.when(leads)
+    def _():
+        forward(1)
+        make(0, *edges[0])
+        for part in range(2, chunks):
+            forward(part)
+        for part in range(1, chunks):
+            make(part, *edges[part])
+
+    last_edges = [(0, up), (up, edges[1][1])] + edges[2:]
+    pl.when(late)(lambda: make_all(order, last_edges, False))
+    for first_part in range(1, chunks):
+        rest_parts = [part for part in order if part != first_part]
+        pl.when(chip == first_part)(
+            lambda parts=[first_part, *rest_parts]: make_all(parts, last_edges, True)
+        )
 
     counts = [count_sends(device, n_dp, chunks) for device in range(n_dp)]
     for pieces in sorted(set(counts)):
@@ -423,7 +450,8 @@
             pltpu.SemaphoreType.REGULAR,
             pltpu.SemaphoreType.REGULAR,
             pltpu.SemaphoreType.DMA((1,)),
-            pltpu.SemaphoreType.DMA((5, CHUNKS)),
+            pltpu.SemaphoreType.DMA((4, CHUNKS)),
+            pltpu.SemaphoreType.DMA((1,)),
             pltpu.SemaphoreType.DMA((2,)),
             pltpu.SemaphoreType.DMA((2,)),
             pltpu.SemaphoreType.DMA((2,)),

time: 16.6 us -> 16.6 us (level)
  no operation moved by 1% of the time
where the time goes in v5:
time: 16.6 us; the launch traced here: 16.5 us
  Pallas kernels  16.5 us (99%)
    pallas_call x1, Pallas kernels, per_device(): pl.pallas_call(functools.partial(gather_kernel, n_dp, n_pipe, 0.2 * math....  13.7 us
    pallas_call x1, Pallas kernels, rows_of(): pl.pallas_call(rows_kernel, out_shape=jax.ShapeDtypeStruct(made.shape, jn...  2.77 us

profile of v5, /device:TPU:0, one launch (start us, length us, event | category | flops | bytes accessed | tf_op | source)
XLA Modules:
  0.0 16.5 jit_solution(11548062486162705268)
XLA Ops:
  0.0 13.7 %gather.1 = (f32[1408,1152]{1,0:T(8,128)S(1)}, f32[1,128]{1,0:T(1,128)S(1)}) custom-call(bf16[64,1152]{1,0:T(8,128)(2,1)} %grad_ref.1, s32[1,64]{1,0:T(1,128)} %bitcast.1), custom_call_target="tpu_custom_call" | custom-call | tf_op jit(solution)/shard_map/gather/pallas_call | solution.py:430
  13.7 2.8 %rows.1 = f32[1408,1152]{1,0:T(8,128)} custom-call(f32[1,128]{1,0:T(1,128)S(1)} %get-tuple-element.7.factor_ref, f32[1408,1152]{1,0:T(8,128)S(1)} %get-tuple-element.8.made_ref), custom_call_target="tpu_custom_call" | custom-call | tf_op jit(solution)/shard_map/rows/pallas_call | solution.py:408
